TPU v7x, 32 devices: a whole 2x2x4 slice. The times are simulated.
32 devices in a mesh: band: 4 (over y, core), col: 8 (over z, x).
Axes of the slice: x: 2, y: 2, z: 4, core: 2. Of those that a mesh axis runs over, the one named last changes fastest.
Arguments:
- source: bfloat16 [6, 524288], P(None, ('band', 'col')), may hold values from -6 to 6
- weights: bfloat16 [8192, 128, 128], P(('band', 'col')), may hold values from -0.5 to 0.5
- source_block: int32 [8192], P(('band', 'col')), may hold values from 0 to 127
- owner_device: int32 [8192, 1], P(('band', 'col')), may hold values from 0 to 31, as said below
- target_tile: int32 [8192], P(('band', 'col')), may hold values from 0 to 112, as said below
- cutoff: int32 [64], P(('band', 'col')), may hold values from 1 to 511
Outputs:
- remapped: float32 [6, 64, 7200], P(None, 'band', 'col')
- filtered: float32 [6, 64, 7200], P(None, 'band', 'col')
Inputs may be any that keep to these rules, and one draw needn't show every extreme that they name: `owner_device`: owners are numbered band index times 8 plus col index. A device's blocks go only to owners in its own band or in the bands next to it. Among the 256 blocks of one device at most 24 share an owner; in every device exactly 24 do for some owner of its own band, and exactly 24 for some owner of each band next to its own; every device sends at least 15 blocks to each owner of its own band. `target_tile`: every tile of every owner receives at least one block.
All inputs are finite; a program needn't handle non-finite values.
Results may differ from a plain program's by a relative error of at most 0.0003.
Values sent between devices are 32-bit elements; how exact they have to be, the bound alone decides.
A program may use at most 64 MiB of HBM per device.

v0:
```python
import jax
import jax.numpy as jnp
from jax import lax
from jax.sharding import PartitionSpec as P

NLON = 7200
KW = 512


TWO_PI = 6.283185307179586


def extended(array, sides, width):
    for axis, dim in sides:
        size, length = (lax.axis_size(axis), array.shape[dim])
        up = [(i, (i + 1) % size) for i in range(size - 1)]
        down = [(j, i) for i, j in up]
        last = lax.slice_in_dim(array, length - width, length, axis=dim)
        leading = lax.slice_in_dim(array, 0, width, axis=dim)
        before = lax.ppermute(last, axis, up)
        after = lax.ppermute(leading, axis, down)
        array = jnp.concatenate([before, array, after], axis=dim)
    return array


def zonal_table(start_index, length, period, wave_count):
    positions = start_index + lax.broadcasted_iota(jnp.int32, (length, wave_count), 0)
    wave_index = lax.broadcasted_iota(jnp.int32, (length, wave_count), 1)
    phases = positions * wave_index % period
    angles = phases.astype(jnp.float32) * (TWO_PI / period)
    return jnp.concatenate([jnp.cos(angles), jnp.sin(angles)], axis=1)


def spectral_weights(cutoffs, wave_count, period):
    wave_index = lax.broadcasted_iota(jnp.int32, (cutoffs.shape[0], wave_count), 1)
    scaled = jnp.where(wave_index == 0, 1.0, 2.0) / period
    retained = jnp.where(wave_index <= cutoffs[:, None], scaled, 0.0).astype(jnp.float32)
    return jnp.concatenate([retained, retained], axis=1)


def local(source, weights, source_block, owner_device, target_tile, cutoff):
    col_count = lax.axis_size("col")
    levels = source.shape[0]
    block_count = weights.shape[0]
    block_width = weights.shape[1]
    lat_here = cutoff.shape[0]
    lat_band = lat_here * col_count
    longitudes_here = NLON // col_count
    cell_count = lat_band * longitudes_here
    tile_count = (cell_count + block_width - 1) // block_width
    regular = (tile_count + col_count - 1) // col_count
    capacity = regular + max(
        1, (block_count - col_count * regular + 2 * col_count - 1) // (2 * col_count)
    )
    slot_total = 3 * col_count * capacity
    blocks_here = source.reshape(levels, -1, block_width)
    picked = jnp.take(blocks_here, source_block, axis=1)
    partial_value = jnp.einsum("lnb,nbt->nlt", picked, weights, preferred_element_type=jnp.float32)
    tile_rows = jnp.broadcast_to(
        target_tile.astype(jnp.float32)[:, None, None], (block_count, 1, block_width)
    )
    tagged = jnp.concatenate([partial_value, tile_rows], axis=1)
    owners = owner_device[:, 0]
    owner_band = owners // col_count
    owner_col = owners % col_count
    offset = owner_band - lax.axis_index("band") + 1
    row_index = lax.broadcasted_iota(jnp.int32, (block_count, block_count), 0)
    column_index = lax.broadcasted_iota(jnp.int32, (block_count, block_count), 1)
    earlier = (owners[None, :] == owners[:, None]) & (column_index < row_index)
    rank_within = jnp.sum(earlier.astype(jnp.int32), axis=1)
    slot_index = (offset * col_count + owner_col) * capacity + rank_within
    placing = lax.broadcasted_iota(jnp.int32, (slot_total, block_count), 0) == slot_index[None, :]
    outgoing = jnp.dot(
        placing.astype(jnp.float32),
        tagged.reshape(block_count, (levels + 1) * block_width),
        precision=lax.Precision.HIGHEST,
        preferred_element_type=jnp.float32,
    )
    outgoing = outgoing.reshape(3, col_count, capacity, levels + 1, block_width)
    rimmed = extended(jnp.stack([outgoing[0], outgoing[2]]), (("band", 0),), 1)
    arranged = jnp.stack([rimmed[0], outgoing[1], rimmed[3]])
    received = lax.all_to_all(arranged, "col", split_axis=1, concat_axis=1, tiled=True)
    slot_rows = received.reshape(-1, levels + 1, block_width)
    slot_owned = slot_rows[:, levels, 0].astype(jnp.int32)
    slot_data = slot_rows[:, :levels, :].reshape(-1, levels * block_width)
    chooser = (
        lax.broadcasted_iota(jnp.int32, (tile_count, slot_owned.shape[0]), 0) == slot_owned[None, :]
    ).astype(jnp.float32)
    summed = jnp.dot(
        chooser, slot_data, precision=lax.Precision.HIGHEST, preferred_element_type=jnp.float32
    )
    summed = jnp.transpose(summed.reshape(tile_count, levels, block_width), (1, 0, 2)).reshape(
        levels, tile_count * block_width
    )
    remapped = summed[:, :cell_count].reshape(levels, lat_band, longitudes_here)
    retained = spectral_weights(cutoff, KW, NLON)
    local_table = zonal_table(lax.axis_index("col") * longitudes_here, longitudes_here, NLON, KW)
    partial_spectra = jnp.dot(
        remapped.reshape(levels * lat_band, longitudes_here),
        local_table,
        precision=lax.Precision.HIGHEST,
        preferred_element_type=jnp.float32,
    )
    partial_spectra = partial_spectra.reshape(levels, lat_band, 2 * KW)
    spectrum = lax.psum_scatter(partial_spectra, "col", scatter_dimension=1, tiled=True)
    spectrum = spectrum * retained[None]
    band_spectra = lax.all_gather(spectrum, "col", axis=1, tiled=True)
    filtered = jnp.dot(
        band_spectra.reshape(levels * lat_band, 2 * KW),
        local_table.T,
        precision=lax.Precision.HIGHEST,
        preferred_element_type=jnp.float32,
    )
    filtered = filtered.reshape(levels, lat_band, longitudes_here)
    return (remapped, filtered)


def solution(mesh):
    in_specs = (
        P(None, ("band", "col")),
        P(("band", "col"), None, None),
        P(("band", "col")),
        P(("band", "col"), None),
        P(("band", "col")),
        P(("band", "col")),
    )
    out_specs = (P(None, "band", "col"), P(None, "band", "col"))
    return jax.shard_map(local, mesh=mesh, in_specs=in_specs, out_specs=out_specs, check_vma=False)
```

profile of v0, /device:TPU:4, one launch (start us, length us, event | category | flops | bytes accessed | tf_op | source)
XLA Modules:
  0.0 206.9 jit_solution(2805658013106343612)
XLA Ops:
  7.2 0.0 copy-start
  7.2 0.7 compare_and_fusion
  7.9 0.7 compare_select_fusion.1
  8.6 0.9 convert_reduce_fusion
  9.5 0.7 convert_element_type.22
  10.2 0.0 copy-done
  10.2 0.8 gather_fusion
  11.0 4.7 %fusion.12 = f32[256,6,128]{2,1,0:T(8,128)S(1)} fusion(bf16[256,128,128]{2,1,0:T(8,128)(2,1)} %param.7, bf16[256,6,128]{2,1,0:T(8,128)(2,1)S(1)} %gather_fusion, pred[256]{0:T(512)(128)(4,1)S(1)} %compare_and_fusion), kind=kOutput, calls=%fused_computation.20 | convolution fusion | flops 50528256 | bytes 9568512 | tf_op jit(solution)/shard_map/lnb,nbt->nlt/dot_general | solution.py:58
  15.8 0.3 broadcast_in_dim.37
  16.1 0.0 copy-start.2
  16.1 0.2 pad_maximum_fusion.1
  16.4 0.4 copy.32
  16.7 0.1 copy-done.2
  16.8 1.2 fusion.11
  18.0 0.1 fusion.29
  18.2 0.1 slice.28
  18.3 0.1 copy.33
  18.4 1.9 collective-permute-start
  20.3 0.1 slice.32
  20.4 0.1 copy.34
  20.6 3.6 %collective-permute-start.1 = (f32[1,8,24,7,128]{4,2,3,1,0:T(8,128)S(1)}, f32[1,8,24,7,128]{4,2,3,1,0:T(8,128)}, u32[]{:S(2)}, u32[]{:S(2)}) collective-permute-start(f32[1,8,24,7,128]{4,2,3,1,0:T(8,128)S(1)} %copy.34), channel_id=1, source_target_pairs={{8,0},{16,8},{24,16},{9,1},{17,9},{25,17},{10,2},{18,10},{26,18},{... | collective-permute-start | bytes 2064392 | tf_op jit(solution)/shard_map/ppermute | solution.py:21
  24.2 0.1 slice.30
  24.3 6.4 %collective-permute-done = f32[1,8,24,7,128]{4,2,3,1,0:T(8,128)} collective-permute-done((f32[1,8,24,7,128]{4,2,3,1,0:T(8,128)S(1)}, f32[1,8,24,7,128]{4,2,3,1,0:T(8,128)}, u32[]{:S(2)}, u32[]{:S(2)}) %collective-permute-start) | collective-permute-done | bytes 688160 | tf_op jit(solution)/shard_map/ppermute | solution.py:20
  30.8 1.2 copy.35
  32.0 0.7 collective-permute-done.1
  32.7 1.2 copy.36
  33.9 0.2 pad_maximum_fusion
  34.2 1.7 copy.37
  35.8 0.0 copy-start.4
  35.8 5.9 %all-to-all-start = ((f32[3,8,24,7,128]{4,2,3,0,1:T(8,128)}), f32[3,8,24,7,128]{4,2,3,0,1:T(8,128)}, u32[]{:S(2)}, u32[]{:S(2)}) async-start(f32[3,8,24,7,128]{4,2,3,0,1:T(8,128)} %copy.37), calls=%async_computation | async-start | bytes 4128768 | tf_op jit(solution)/shard_map/all_to_all | solution.py:82
  41.8 0.0 all-reduce.3.cloned.1.call-start
  41.8 0.0 copy-done.4
  41.8 0.6 dynamic-slice
  43.1 8.8 %fusion.7 = (f32[900,512]{1,0:T(8,128)S(1)}, f32[900,512]{1,0:T(8,128)}) fusion(s32[900]{0:T(1024)S(1)} %iota_add_fusion), kind=kLoop, calls=%fused_computation.12 | loop fusion | flops 4147200 | bytes 3690000 | tf_op jit(solution)/shard_map/cos | solution.py:31
  51.9 30.5 %all-to-all-done = f32[3,8,24,7,128]{4,2,3,0,1:T(8,128)} async-done(((f32[3,8,24,7,128]{4,2,3,0,1:T(8,128)}), f32[3,8,24,7,128]{4,2,3,0,1:T(8,128)}, u32[]{:S(2)}, u32[]{:S(2)}) %all-to-all-start) | async-done | bytes 2064416 | tf_op jit(solution)/shard_map/all_to_all | solution.py:82
  82.4 1.8 copy.38
  84.2 0.2 fusion.17
  84.3 0.9 fusion.10
  85.3 0.1 copy.52
  85.4 0.3 reshape.113
  85.7 0.0 copy-start.1
  85.7 0.0 copy-start.3
  85.7 4.7 %fusion.1 = f32[6,16,1024]{2,1,0:T(8,128)} fusion(f32[6,16,900]{2,1,0:T(8,128)S(1)} %reshape.113, f32[900,512]{1,0:T(8,128)} %get-tuple-element.6, f32[900,512]{1,0:T(8,128)S(1)} %get-tuple-element.5), kind=kOutput, calls=%fused_computation.3 | convolution fusion | flops 1062604800 | bytes 4425216 | tf_op jit(solution)/shard_map/dot_general | solution.py:98
  90.4 0.0 copy-done.1
  90.4 0.0 all-reduce.3.cloned.1.call-update
  90.4 0.0 copy-done.3
  90.4 0.1 compare_select_fusion
  90.5 71.1 %all-reduce.3.cloned.1.call-done = f32[6,16,1024]{2,1,0:T(8,128)} async-done(((f32[6,16,1024]{2,1,0:T(8,128)}), f32[6,16,1024]{2,1,0:T(8,128)}) %all-reduce.3.cloned.1.call-update) | async-done | bytes 393232
  161.6 0.9 dynamic-slice_multiply_fusion
  162.6 31.8 %all_gather.3 = f32[6,16,1024]{2,0,1:T(8,128)S(1)} all-gather(f32[6,2,1024]{2,0,1:T(8,128)S(1)} %copy.41), channel_id=1, replica_groups=mesh['band'=4,'col'=8] {'col'}, dimensions={1}, use_global_device_ids=true | all-gather | bytes 442368 | tf_op jit(solution)/shard_map/all_gather | solution.py:107
  194.3 5.7 %fusion = f32[6,16,900]{2,1,0:T(8,128)} fusion(f32[900,512]{1,0:T(8,128)} %get-tuple-element.6, f32[900,512]{1,0:T(8,128)S(1)} %get-tuple-element.5, f32[6,16,1024]{2,0,1:T(8,128)S(1)} %all_gather.3), kind=kOutput, calls=%fused_computation.2 | convolution fusion | flops 1062604800 | bytes 4425216 | tf_op jit(solution)/shard_map/dot_general | solution.py:108
  (6 shorter events, 0.1 us)
Async XLA Ops:
  7.2 3.1 %copy-start = (bf16[6,16384]{1,0:T(8,128)(2,1)S(1)}, bf16[6,16384]{1,0:T(8,128)(2,1)}, u32[]{:S(2)}) copy-start(bf16[6,16384]{1,0:T(8,128)(2,1)} %param.6) | copy-start | bytes 589828
  16.1 0.7 copy-start.2
  18.4 12.4 %collective-permute-start = (f32[1,8,24,7,128]{4,2,3,1,0:T(8,128)S(1)}, f32[1,8,24,7,128]{4,2,3,1,0:T(8,128)}, u32[]{:S(2)}, u32[]{:S(2)}) collective-permute-start(f32[1,8,24,7,128]{4,2,3,1,0:T(8,128)S(1)} %copy.33), channel_id=1, source_target_pairs={{0,8},{8,16},{16,24},{1,9},{9,17},{17,25},{2,10},{10,18},{18,26},{... | collective-permute-start | bytes 2064392 | tf_op jit(solution)/shard_map/ppermute | solution.py:20
  20.6 12.1 %collective-permute-start.1 = (f32[1,8,24,7,128]{4,2,3,1,0:T(8,128)S(1)}, f32[1,8,24,7,128]{4,2,3,1,0:T(8,128)}, u32[]{:S(2)}, u32[]{:S(2)}) collective-permute-start(f32[1,8,24,7,128]{4,2,3,1,0:T(8,128)S(1)} %copy.34), channel_id=1, source_target_pairs={{8,0},{16,8},{24,16},{9,1},{17,9},{25,17},{10,2},{18,10},{26,18},{... | collective-permute-start | bytes 2064392 | tf_op jit(solution)/shard_map/ppermute | solution.py:21
  35.8 6.0 %copy-start.4 = (u32[32]{0:T(128)S(1)}, u32[32]{0:T(128)}, u32[]{:S(2)}) copy-start(u32[32]{0:T(128)} %constant.84) | copy-start | bytes 388
  35.8 46.5 %all-to-all-start = ((f32[3,8,24,7,128]{4,2,3,0,1:T(8,128)}), f32[3,8,24,7,128]{4,2,3,0,1:T(8,128)}, u32[]{:S(2)}, u32[]{:S(2)}) async-start(f32[3,8,24,7,128]{4,2,3,0,1:T(8,128)} %copy.37), calls=%async_computation | async-start | bytes 4128768 | tf_op jit(solution)/shard_map/all_to_all | solution.py:82
  41.8 119.8 %all-reduce.3.cloned.1.call-start = ((), (), s32[]{:S(2)}) async-start(), calls=%async_computation.1 | async-start | bytes 786432
  85.7 4.7 %copy-start.1 = (f32[6,16,900]{2,1,0:T(8,128)}, f32[6,16,900]{2,1,0:T(8,128)S(1)}, u32[]{:S(2)}) copy-start(f32[6,16,900]{2,1,0:T(8,128)S(1)} %reshape.113) | copy-start | bytes 1036804
  85.7 4.7 %copy-start.3 = (s32[2]{0:T(128)S(1)}, s32[2]{0:T(128)}, u32[]{:S(2)}) copy-start(s32[2]{0:T(128)} %param.11) | copy-start | bytes 28
Sparse Core Ops, SparseCore 0:
  90.5 70.9 all-reduce.2
where the time goes:
time: 209 us; the launch traced here: 207 us
  waiting for transfers between devices  109 us (52%)
  blocking collectives  31.8 us (15%)
  matrix products  17.2 us (8%)
  between operations  14.9 us (7%)
  other arithmetic  13.6 us (7%)
  starting transfers between devices  11.5 us (6%)
  local copies, waits for them, and re-layouts  9.29 us (4%)
    unnamed x2, waiting for transfers between devices  71.1 us
    all_gather x1, blocking collectives, local(): band_spectra = lax.all_gather(spectrum, 'col', axis=1, tiled=True)  31.8 us
    all_to_all x1, waiting for transfers between devices, local(): lax.all_to_all(arranged, 'col', split_axis=1, concat_axis=1, tiled=True)  30.5 us
    cos x1, other arithmetic, zonal_table(): return jnp.concatenate([jnp.cos(angles), jnp.sin(angles)], axis=1)  8.82 us
    ppermute x1, waiting for transfers between devices, extended(): before = lax.ppermute(last, axis, up)  6.42 us
    all_to_all x1, starting transfers between devices, local(): lax.all_to_all(arranged, 'col', split_axis=1, concat_axis=1, tiled=True)  5.94 us
    dot_general x1, matrix products, local(): jnp.dot(band_spectra.reshape(levels * lat_band, 2 * KW), local_table.T, p...  5.74 us
    dot_general x1, matrix products, local(): jnp.einsum('lnb,nbt->nlt', picked, weights, preferred_element_type=jnp.fl...  4.73 us
  transfers between devices with their start and end apart: 4, of which 4 were waited for; matrix products, arithmetic and copies ran while one was open for 5% of the time, Pallas kernels for 0%

commit v1 on v0

v1 whole, which is shorter than its diff:
```python
import functools

import jax
import jax.numpy as jnp
from jax import lax
from jax.experimental import pallas as pl
from jax.experimental.pallas import tpu as pltpu
from jax.sharding import PartitionSpec as P

NLON = 7200
KW = 512
LANES = 128
STEP = 16
TWO_PI = 6.283185307179586
MESH = pl.DeviceIdType.MESH
F32 = jnp.float32
BF16 = jnp.bfloat16


def round_up(value, multiple):
    return (value + multiple - 1) // multiple * multiple


def split(value):
    high = value.astype(BF16)
    return high, (value - high.astype(F32)).astype(BF16)


def dot(left, right, left_dim=1, right_dim=0):
    return lax.dot_general(
        left, right, (((left_dim,), (right_dim,)), ((), ())), preferred_element_type=F32
    )


def exchange_kernel(
    bands, cols, levels, capacity, wave_count,
    partial, owner_row, owner_column, tile_row, fine, coarse,
    sums, table_high, table_low,
    slab, recv, send_sem, recv_sem,
):
    band, col = lax.axis_index("band"), lax.axis_index("col")
    blocks = partial.shape[0]
    rows = levels * capacity
    owners = owner_row[...]
    sublane = lax.broadcasted_iota(jnp.int32, (blocks, blocks), 0)
    lane = lax.broadcasted_iota(jnp.int32, (blocks, blocks), 1)
    earlier = (owner_column[...] == owners) & (sublane < lane)
    rank = jnp.sum(earlier.astype(jnp.int32), axis=0, keepdims=True)
    place = owners - (band - 1) * cols
    slot = place * capacity + rank
    data = jnp.concatenate([partial[:, level, :] for level in range(levels)], axis=1)
    stacked = jnp.concatenate(split(data), axis=0)
    slot_lane = lax.broadcasted_iota(jnp.int32, (LANES, blocks), 0)
    tile_at = jnp.where(slot_lane == rank, tile_row[...], 0).astype(F32).astype(BF16)

    def valid(offset):
        target = band + (offset - 1)
        return (target >= 0) & (target < bands)

    def send(offset):
        group = cols * capacity
        ids = lax.broadcasted_iota(jnp.int32, (group, blocks), 0) + offset * group
        placing = (ids == slot).astype(F32).astype(BF16)
        placed = dot(jnp.concatenate([placing, placing], axis=1), stacked)
        place_ids = lax.broadcasted_iota(jnp.int32, (cols, blocks), 0) + offset * cols
        chosen = (place_ids == place).astype(F32).astype(BF16)
        tags = dot(chosen, tile_at, 1, 1)
        here = pl.ds(offset * cols, cols)
        for level in range(levels):
            piece = placed[:, level * LANES : (level + 1) * LANES]
            slab[here, level * capacity : (level + 1) * capacity, :] = piece.reshape(
                cols, capacity, LANES
            )
        slab[here, rows : rows + 8, :] = jnp.broadcast_to(tags[:, None, :], (cols, 8, LANES))

        def one(step, carry):
            to = lax.rem(col + cols // 2 + step, cols)

            def start_remote():
                pltpu.make_async_remote_copy(
                    src_ref=slab.at[offset * cols + to],
                    dst_ref=recv.at[(2 - offset) * cols + col],
                    send_sem=send_sem.at[offset],
                    recv_sem=recv_sem.at[2 - offset],
                    device_id=(band + (offset - 1), to),
                    device_id_type=MESH,
                ).start()

            if offset == 1:
                pl.when(to != col)(start_remote)
            else:
                start_remote()
            return carry

        lax.fori_loop(0, cols, one, 0)
        if offset == 1:
            pltpu.make_async_copy(
                slab.at[cols + col], recv.at[cols + col], recv_sem.at[1]
            ).start()

    for offset in (0, 2, 1):
        pl.when(valid(offset))(functools.partial(send, offset))

    def table_step(step, carry):
        pair = coarse[step]
        cos_base, sin_base = pair[0:1], pair[1:2]
        cos_fine, sin_fine = fine[0], fine[1]
        at = pl.ds(pl.multiple_of(step * STEP, STEP), STEP)
        for start, value in (
            (0, cos_base * cos_fine - sin_base * sin_fine),
            (wave_count, sin_base * cos_fine + cos_base * sin_fine),
        ):
            high, low = split(value)
            table_high[at, start : start + wave_count] = high
            table_low[at, start : start + wave_count] = low
        return carry

    lax.fori_loop(0, coarse.shape[0], table_step, 0)

    tiles = sums.shape[1]
    sums[...] = jnp.zeros_like(sums)

    def receive(offset):
        here = pl.ds(offset * cols, cols)
        pltpu.make_async_copy(slab.at[here], recv.at[here], recv_sem.at[offset]).wait()
        tags = jnp.transpose(recv[here, rows, :])
        wide = lax.broadcasted_iota(jnp.int32, (capacity, tiles), 1).astype(F32)
        chooser = jnp.concatenate(
            [
                (tags[:capacity, source : source + 1] == wide).astype(F32)
                for source in range(cols)
            ],
            axis=0,
        )
        chooser = jnp.transpose(chooser).astype(BF16)
        arrived = jnp.concatenate(
            [
                recv[here, level * capacity : (level + 1) * capacity, :].reshape(
                    cols * capacity, LANES
                )
                for level in range(levels)
            ],
            axis=1,
        )
        high, low = split(arrived)
        total = dot(chooser, high) + dot(chooser, low)
        for level in range(levels):
            sums[level] += total[:, level * LANES : (level + 1) * LANES]

    for offset in (1, 0, 2):
        pl.when(valid(offset))(functools.partial(receive, offset))

    def drain(offset):
        first = offset * cols
        count = cols - 1 if offset == 1 else cols
        here = pl.ds(first, count)
        pltpu.make_async_copy(slab.at[here], recv.at[here], send_sem.at[offset]).wait()

    for offset in range(3):
        pl.when(valid(offset))(functools.partial(drain, offset))


def exchange(mesh, capacity, tiles, long_pad, partial, owner, tile, fine, coarse):
    bands, cols = mesh.shape["band"], mesh.shape["col"]
    blocks, levels, width = partial.shape
    wave_count = fine.shape[-1]
    slab_rows = levels * capacity + 8
    vmem = pl.BlockSpec(memory_space=pltpu.VMEM)
    return pl.pallas_call(
        functools.partial(exchange_kernel, bands, cols, levels, capacity, wave_count),
        out_shape=(
            jax.ShapeDtypeStruct((levels, tiles, width), F32),
            jax.ShapeDtypeStruct((long_pad, 2 * wave_count), BF16),
            jax.ShapeDtypeStruct((long_pad, 2 * wave_count), BF16),
        ),
        in_specs=[vmem] * 6,
        out_specs=(vmem,) * 3,
        scratch_shapes=[
            pltpu.VMEM((3 * cols, slab_rows, width), F32),
            pltpu.VMEM((3 * cols, slab_rows, width), F32),
            pltpu.SemaphoreType.DMA((3,)),
            pltpu.SemaphoreType.DMA((3,)),
        ],
        compiler_params=pltpu.CompilerParams(has_side_effects=True, vmem_limit_bytes=48 << 20),
    )(partial, owner.reshape(1, blocks), owner, tile.reshape(1, blocks), fine, coarse)


def filter_kernel(
    cols, group, lat_here, period, wave_count,
    cutoff, field, table_high, table_low,
    out,
    spectra, arrived, scaled, gathered, send_sem, recv_sem, send_sem2, recv_sem2,
):
    band, col = lax.axis_index("band"), lax.axis_index("col")
    rows = cols * group
    width_tiles = spectra.shape[1]
    high, low = split(field[...])
    both = dot(jnp.concatenate([high, low], axis=0), table_high[...])
    spectrum = both[:rows] + both[rows:] + dot(high, table_low[...])
    for tile in range(width_tiles):
        spectra[:, tile, :] = spectrum[:, tile * LANES : (tile + 1) * LANES]

    def mine(ref, index):
        return ref.at[pl.ds(index * group, group)]

    def scatter(step, carry):
        to = lax.rem(col + cols // 2 + step, cols)

        def start_remote():
            pltpu.make_async_remote_copy(
                src_ref=mine(spectra, to),
                dst_ref=mine(arrived, col),
                send_sem=send_sem,
                recv_sem=recv_sem,
                device_id=(band, to),
                device_id_type=MESH,
            ).start()

        pl.when(to != col)(start_remote)
        return carry

    lax.fori_loop(0, cols, scatter, 0)
    pltpu.make_async_copy(mine(spectra, col), mine(arrived, col), recv_sem).start()
    j = (
        lax.broadcasted_iota(jnp.int32, (width_tiles, LANES), 0) * LANES
        + lax.broadcasted_iota(jnp.int32, (width_tiles, LANES), 1)
    )
    wave = jnp.where(j >= wave_count, j - wave_count, j)
    weight = jnp.where(wave == 0, 1.0, 2.0) / period
    gains = [jnp.where(wave <= cutoff[lat], weight, 0.0).astype(F32) for lat in range(lat_here)]
    pltpu.make_async_copy(spectra, arrived, recv_sem).wait()
    for row in range(group):
        total = arrived[row]
        for source in range(1, cols):
            total += arrived[source * group + row]
        scaled[row] = total * gains[row % lat_here]

    def spread(step, carry):
        to = lax.rem(col + cols // 2 + step, cols)

        def start_remote():
            pltpu.make_async_remote_copy(
                src_ref=scaled,
                dst_ref=mine(gathered, col),
                send_sem=send_sem2,
                recv_sem=recv_sem2,
                device_id=(band, to),
                device_id_type=MESH,
            ).start()

        pl.when(to != col)(start_remote)
        return carry

    lax.fori_loop(0, cols, spread, 0)
    pltpu.make_async_copy(scaled, mine(gathered, col), recv_sem2).start()
    pltpu.make_async_copy(spectra, gathered, recv_sem2).wait()
    spectrum = jnp.concatenate([gathered[:, tile, :] for tile in range(width_tiles)], axis=1)
    high, low = split(spectrum)
    both = dot(jnp.concatenate([high, low], axis=0), table_high[...], 1, 1)
    out[...] = both[:rows] + both[rows:] + dot(high, table_low[...], 1, 1)
    others = pl.ds(0, (cols - 1) * group)
    pltpu.make_async_copy(spectra.at[others], arrived.at[others], send_sem).wait()
    pltpu.make_async_copy(spectra.at[others], arrived.at[others], send_sem2).wait()


def zonal_filter(mesh, group, cutoff, field, table_high, table_low):
    cols = mesh.shape["col"]
    rows, long_pad = field.shape
    waves = table_high.shape[1]
    shape = (rows, waves // LANES, LANES)
    vmem = pl.BlockSpec(memory_space=pltpu.VMEM)
    return pl.pallas_call(
        functools.partial(filter_kernel, cols, group, cutoff.shape[0], NLON, waves // 2),
        out_shape=jax.ShapeDtypeStruct((rows, long_pad), F32),
        in_specs=[pl.BlockSpec(memory_space=pltpu.SMEM)] + [vmem] * 3,
        out_specs=vmem,
        scratch_shapes=[
            pltpu.VMEM(shape, F32),
            pltpu.VMEM(shape, F32),
            pltpu.VMEM((group,) + shape[1:], F32),
            pltpu.VMEM(shape, F32),
            pltpu.SemaphoreType.DMA,
            pltpu.SemaphoreType.DMA,
            pltpu.SemaphoreType.DMA,
            pltpu.SemaphoreType.DMA,
        ],
        compiler_params=pltpu.CompilerParams(has_side_effects=True, vmem_limit_bytes=48 << 20),
    )(cutoff, field, table_high, table_low)


def cos_sin(positions):
    wave_index = lax.broadcasted_iota(jnp.int32, (positions.shape[0], KW), 1)
    phases = positions[:, None] * wave_index % NLON
    angles = phases.astype(F32) * (TWO_PI / NLON)
    return jnp.cos(angles), jnp.sin(angles)


def local(mesh, source, weights, source_block, owner_device, target_tile, cutoff):
    cols = mesh.shape["col"]
    levels = source.shape[0]
    block_count, block_width = weights.shape[:2]
    lat_here = cutoff.shape[0]
    lat_band = lat_here * cols
    longitudes = NLON // cols
    cell_count = lat_band * longitudes
    tile_count = (cell_count + block_width - 1) // block_width
    regular = (tile_count + cols - 1) // cols
    capacity = regular + max(1, (block_count - cols * regular + 2 * cols - 1) // (2 * cols))
    capacity = round_up(capacity, 8)
    tiles = round_up(tile_count, LANES)
    long_pad = round_up(longitudes, LANES)
    fine = jnp.stack(cos_sin(jnp.arange(STEP, dtype=jnp.int32)))
    starts = lax.axis_index("col") * longitudes + STEP * jnp.arange(long_pad // STEP, dtype=jnp.int32)
    coarse = jnp.stack(cos_sin(starts), axis=1)

    blocks_here = source.reshape(levels, -1, block_width)
    picked = jnp.take(blocks_here, source_block, axis=1)
    partial = jnp.einsum("lnb,nbt->nlt", picked, weights, preferred_element_type=F32)
    sums, table_high, table_low = exchange(
        mesh, capacity, tiles, long_pad, partial, owner_device, target_tile, fine, coarse
    )
    remapped = sums.reshape(levels, -1)[:, :cell_count].reshape(levels, lat_band, longitudes)
    group = levels * lat_here
    field = remapped.reshape(levels, cols, lat_here, longitudes).transpose(1, 0, 2, 3)
    field = field.reshape(cols * group, longitudes)
    field = jnp.pad(field, ((0, 0), (0, long_pad - longitudes)))
    filtered = zonal_filter(mesh, group, cutoff, field, table_high, table_low)
    filtered = filtered[:, :longitudes].reshape(cols, levels, lat_here, longitudes)
    filtered = filtered.transpose(1, 0, 2, 3).reshape(levels, lat_band, longitudes)
    return remapped, filtered


def solution(mesh):
    in_specs = (
        P(None, ("band", "col")),
        P(("band", "col"), None, None),
        P(("band", "col")),
        P(("band", "col"), None),
        P(("band", "col")),
        P(("band", "col")),
    )
    out_specs = (P(None, "band", "col"), P(None, "band", "col"))
    return jax.shard_map(
        functools.partial(local, mesh),
        mesh=mesh,
        in_specs=in_specs,
        out_specs=out_specs,
        check_vma=False,
    )
```

time: 209 us -> 95.9 us (0.46)
  waiting for transfers between devices: 109 us -> 0 us
  Pallas kernels: 0 us -> 74 us
  blocking collectives: 31.8 us -> 0 us
  between operations: 14.9 us -> 0.81 us
  matrix products: 17.2 us -> 4.73 us
  starting transfers between devices: 11.5 us -> 0 us
  other arithmetic: 13.6 us -> 5.7 us
    pallas_call x0 -> x2, Pallas kernels: none -> 74 us  [the longest x1 46.2 us: exchange(): pl.pallas_call(functools.partial(exchange_kernel, bands, cols, levels, ca...]
    unnamed x2 -> x0, waiting for transfers between devices: 71.1 us -> none
    all_gather x1 -> x0, blocking collectives: 31.8 us -> none  [local(): band_spectra = lax.all_gather(spectrum, 'col', axis=1, tiled=True)]
    all_to_all x1 -> x0, waiting for transfers between devices: 30.5 us -> none  [local(): lax.all_to_all(arranged, 'col', split_axis=1, concat_axis=1, tiled=True)]
    dot_general x5 -> x1, matrix products: 17.2 us -> 4.73 us  [local(): jnp.einsum('lnb,nbt->nlt', picked, weights, preferred_element_type=F32)]
    ppermute x2 -> x0, waiting for transfers between devices: 7.08 us -> none  [the longest x1 6.42 us: extended(): before = lax.ppermute(last, axis, up)]
    all_to_all x1 -> x0, starting transfers between devices: 5.94 us -> none  [local(): lax.all_to_all(arranged, 'col', split_axis=1, concat_axis=1, tiled=True)]
    ppermute x2 -> x0, starting transfers between devices: 5.56 us -> none  [the longest x1 3.64 us: extended(): after = lax.ppermute(leading, axis, down)]
  transfers between devices with their start and end apart: 4 -> 0, of which waited for: 4 -> 0; matrix products, arithmetic and copies ran while one was open for 5% -> 0% of each run, Pallas kernels for 0% -> 0%
where the time goes in v1:
time: 95.9 us; the launch traced here: 94.2 us
  Pallas kernels  74 us (77%)
  local copies, waits for them, and re-layouts  8.89 us (9%)
  other arithmetic  5.7 us (6%)
  matrix products  4.73 us (5%)
    pallas_call x1, Pallas kernels, exchange(): pl.pallas_call(functools.partial(exchange_kernel, bands, cols, levels, ca...  46.2 us
    pallas_call x1, Pallas kernels, zonal_filter(): pl.pallas_call(functools.partial(filter_kernel, cols, group, cutoff.shape...  27.9 us
    unnamed x14, local copies, waits for them, and re-layouts  4.9 us
    dot_general x1, matrix products, local(): jnp.einsum('lnb,nbt->nlt', picked, weights, preferred_element_type=F32)  4.73 us
    cos x1, other arithmetic, cos_sin(): return (jnp.cos(angles), jnp.sin(angles))  3.78 us

profile of v1, /device:TPU:4, one launch (start us, length us, event | category | flops | bytes accessed | tf_op | source)
XLA Modules:
  0.0 94.2 jit_solution(18376817784771512919)
XLA Ops:
  0.6 0.0 copy-start
  0.6 0.0 copy-start.3
  0.7 0.0 copy-start.4
  0.7 0.9 copy-done
  1.6 0.7 compare_and_fusion
  2.3 0.7 compare_select_fusion
  3.0 0.1 fusion.13
  3.1 0.1 fusion.5
  3.3 0.8 copy.14.owner_column
  4.1 3.8 %fusion.17 = (f32[64,1,512]{2,1,0:T(1,128)S(1)}, f32[64,1,512]{2,1,0:T(1,128)S(1)}) fusion(f32[64,1,512]{2,0,1:T(8,128)S(1)} %fusion.5), kind=kLoop, calls=%fused_computation.26 | loop fusion | flops 32768 | bytes 393216 | tf_op jit(solution)/shard_map/cos | solution.py:295
  7.9 0.2 pad_maximum_fusion.coarse
  8.1 0.8 gather_fusion
  8.9 0.0 copy-start.5
  9.0 4.7 %fusion.partial = f32[256,6,128]{2,1,0:T(8,128)S(1)} fusion(bf16[256,128,128]{2,1,0:T(8,128)(2,1)} %param.7, bf16[256,6,128]{2,1,0:T(8,128)(2,1)S(1)} %gather_fusion, pred[256]{0:T(512)(128)(4,1)S(1)} %compare_and_fusion), kind=kOutput, calls=%fused_computation.2 | convolution fusion | flops 50528256 | bytes 9568512 | tf_op jit(solution)/shard_map/lnb,nbt->nlt/dot_general | solution.py:318
  13.7 0.0 copy-done.3
  13.7 0.0 copy-done.4
  13.7 46.2 %shard_map.77 = (f32[6,128,128]{2,1,0:T(8,128)S(1)}, bf16[1024,1024]{1,0:T(8,128)(2,1)S(1)}, bf16[1024,1024]{1,0:T(8,128)(2,1)S(1)}) custom-call(f32[256,6,128]{2,1,0:T(8,128)S(1)} %fusion.partial, s32[1,256]{1,0:T(1,128)S(1)} %bitcast.17, s32[256,1]{1,0:T(8,128)S(1)} %copy.14.owner_column, s32[1,256]{1,0:T(1,128)S(1)} %bitcast.18, ...), custom_call_target="tpu_custom_call" | custom-call | tf_op jit(solution)/shard_map/pallas_call | solution.py:169
  59.9 0.0 copy-start.1
  59.9 1.3 %copy-done.1 = bf16[1024,1024]{1,0:T(8,128)(2,1)} copy-done((bf16[1024,1024]{1,0:T(8,128)(2,1)}, bf16[1024,1024]{1,0:T(8,128)(2,1)S(1)}, u32[]{:S(2)}) %copy-start.1) | copy-done | bytes 2097176
  61.2 0.2 copy.24
  61.5 0.4 reshape_reshape.3
  61.9 1.1 %reshape.163 = f32[6,16,900]{2,1,0:T(8,128)} reshape(f32[6,14400]{1,0:T(8,128)S(1)} %slice.10) | data formatting | bytes 691200 | tf_op jit(solution)/shard_map/reshape | solution.py:322
  63.0 0.3 reshape.164
  63.4 0.0 copy-done.5
  63.4 0.0 copy-start.2
  63.4 1.6 %copy-done.2 = bf16[1024,1024]{1,0:T(8,128)(2,1)S(1)} copy-done((bf16[1024,1024]{1,0:T(8,128)(2,1)S(1)}, bf16[1024,1024]{1,0:T(8,128)(2,1)}, u32[]{:S(2)}) %copy-start.2) | copy-done | bytes 2097176
  65.0 27.9 %shard_map.78 = f32[96,1024]{1,0:T(8,128)S(1)} custom-call(s32[2]{0:T(128)S(1)} %copy-done.5, f32[96,1024]{1,0:T(8,128)S(1)} %pad.4.field, bf16[1024,1024]{1,0:T(8,128)(2,1)S(1)} %get-tuple-element.6.table_high, bf16[1024,1024]{1,0:T(8,128)(2,1)S(1)} %copy-done.2), custom_call_target="tpu_custom_call" | custom-call | tf_op jit(solution)/shard_map/pallas_call | solution.py:272
  92.8 0.2 reshape.165
  93.1 1.0 %reshape.166 = f32[6,16,900]{2,1,0:T(8,128)} reshape(f32[6,8,2,900]{3,2,1,0:T(2,128)S(1)} %copy.16) | data formatting | bytes 691200 | tf_op jit(solution)/shard_map/reshape | solution.py:329
  (7 shorter events, 0.1 us)
Async XLA Ops:
  0.6 1.0 %copy-start = (bf16[6,16384]{1,0:T(8,128)(2,1)S(1)}, bf16[6,16384]{1,0:T(8,128)(2,1)}, u32[]{:S(2)}) copy-start(bf16[6,16384]{1,0:T(8,128)(2,1)} %param.6) | copy-start | bytes 589828
  0.6 13.0 %copy-start.3 = (s32[256,1]{0,1:T(1,128)S(1)}, s32[256,1]{0,1:T(1,128)}, u32[]{:S(2)}) copy-start(s32[256,1]{0,1:T(1,128)} %param.9) | copy-start | bytes 3076
  0.7 13.0 %copy-start.4 = (s32[256]{0:T(256)S(1)}, s32[256]{0:T(256)}, u32[]{:S(2)}) copy-start(s32[256]{0:T(256)} %param.10) | copy-start | bytes 3076
  8.9 54.4 %copy-start.5 = (s32[2]{0:T(128)S(1)}, s32[2]{0:T(128)}, u32[]{:S(2)}) copy-start(s32[2]{0:T(128)} %cutoff.1) | copy-start | bytes 28
  59.9 1.3 %copy-start.1 = (bf16[1024,1024]{1,0:T(8,128)(2,1)}, bf16[1024,1024]{1,0:T(8,128)(2,1)S(1)}, u32[]{:S(2)}) copy-start(bf16[1024,1024]{1,0:T(8,128)(2,1)S(1)} %get-tuple-element.7.table_low) | copy-start | bytes 6291460
  63.4 1.6 %copy-start.2 = (bf16[1024,1024]{1,0:T(8,128)(2,1)S(1)}, bf16[1024,1024]{1,0:T(8,128)(2,1)}, u32[]{:S(2)}) copy-start(bf16[1024,1024]{1,0:T(8,128)(2,1)} %copy-done.1) | copy-start | bytes 6291460

commit v2 on v1

v2 whole, which is shorter than its diff:
```python
import functools

import jax
import jax.numpy as jnp
import numpy as np
from jax import lax
from jax.experimental import pallas as pl
from jax.experimental.pallas import tpu as pltpu
from jax.sharding import PartitionSpec as P

NLON = 7200
KW = 512
LANES = 128
STEP = 16
MESH = pl.DeviceIdType.MESH
F32 = jnp.float32
BF16 = jnp.bfloat16


def round_up(value, multiple):
    return (value + multiple - 1) // multiple * multiple


def split(value):
    high = value.astype(BF16)
    return high, (value - high.astype(F32)).astype(BF16)


def dot(left, right, left_dim=1, right_dim=0):
    return lax.dot_general(
        left, right, (((left_dim,), (right_dim,)), ((), ())), preferred_element_type=F32
    )


def remap_kernel(
    bands, cols, levels, capacity, wave_count, period, longitudes,
    cutoff, partial, owner_row, owner_column, tile_row, fine, coarse, start,
    remapped, filtered,
    sums, table_high, table_low, rotated, field, slab, recv,
    spectra, arrived, scaled, gathered,
    send_sem, recv_sem, scatter_send, scatter_recv, spread_send, spread_recv,
):
    band, col = lax.axis_index("band"), lax.axis_index("col")
    blocks = partial.shape[0]
    rows = levels * capacity
    owners = owner_row[...]
    sublane = lax.broadcasted_iota(jnp.int32, (blocks, blocks), 0)
    lane = lax.broadcasted_iota(jnp.int32, (blocks, blocks), 1)
    earlier = (owner_column[...] == owners) & (sublane < lane)
    rank = jnp.sum(earlier.astype(jnp.int32), axis=0, keepdims=True)
    place = owners - (band - 1) * cols
    slot = place * capacity + rank
    data = jnp.concatenate([partial[:, level, :] for level in range(levels)], axis=1)
    stacked = jnp.concatenate(split(data), axis=0)
    slot_lane = lax.broadcasted_iota(jnp.int32, (LANES, blocks), 0)
    tile_at = jnp.where(slot_lane == rank, tile_row[...], 0).astype(F32).astype(BF16)

    def valid(offset):
        target = band + (offset - 1)
        return (target >= 0) & (target < bands)

    def to_others(start_copy):
        def one(step, carry):
            to = lax.rem(col + cols // 2 + step, cols)
            pl.when(to != col)(functools.partial(start_copy, to))
            return carry

        lax.fori_loop(0, cols, one, 0)

    def send(offset):
        group = cols * capacity
        ids = lax.broadcasted_iota(jnp.int32, (group, blocks), 0) + offset * group
        placing = (ids == slot).astype(F32).astype(BF16)
        placed = dot(jnp.concatenate([placing, placing], axis=1), stacked)
        place_ids = lax.broadcasted_iota(jnp.int32, (cols, blocks), 0) + offset * cols
        chosen = (place_ids == place).astype(F32).astype(BF16)
        tags = dot(chosen, tile_at, 1, 1)
        here = pl.ds(offset * cols, cols)
        for level in range(levels):
            piece = placed[:, level * LANES : (level + 1) * LANES]
            slab[here, level * capacity : (level + 1) * capacity, :] = piece.reshape(
                cols, capacity, LANES
            )
        slab[here, rows : rows + 8, :] = jnp.broadcast_to(tags[:, None, :], (cols, 8, LANES))

        def start_remote(to):
            pltpu.make_async_remote_copy(
                src_ref=slab.at[offset * cols + to],
                dst_ref=recv.at[(2 - offset) * cols + col],
                send_sem=send_sem.at[offset],
                recv_sem=recv_sem.at[2 - offset],
                device_id=(band + (offset - 1), to),
                device_id_type=MESH,
            ).start()

        to_others(start_remote)
        if offset == 1:
            pltpu.make_async_copy(
                slab.at[cols + col], recv.at[cols + col], recv_sem.at[1]
            ).start()
        else:
            start_remote(col)

    for offset in (0, 2, 1):
        pl.when(valid(offset))(functools.partial(send, offset))

    begin = start[col]
    cos_start, sin_start = begin[0:1], begin[1:2]
    rotated[0] = fine[0] * cos_start - fine[1] * sin_start
    rotated[1] = fine[1] * cos_start + fine[0] * sin_start

    def table_step(step, carry):
        pair = coarse[step]
        cos_base, sin_base = pair[0:1], pair[1:2]
        cos_fine, sin_fine = rotated[0], rotated[1]
        at = pl.ds(pl.multiple_of(step * STEP, STEP), STEP)
        for first, value in (
            (0, cos_base * cos_fine - sin_base * sin_fine),
            (wave_count, sin_base * cos_fine + cos_base * sin_fine),
        ):
            high, low = split(value)
            table_high[at, first : first + wave_count] = high
            table_low[at, first : first + wave_count] = low
        return carry

    lax.fori_loop(0, coarse.shape[0], table_step, 0)

    tiles = sums.shape[1]
    sums[...] = jnp.zeros_like(sums)

    def receive(offset):
        here = pl.ds(offset * cols, cols)
        pltpu.make_async_copy(slab.at[here], recv.at[here], recv_sem.at[offset]).wait()
        tags = jnp.transpose(recv[here, rows, :])
        wide = lax.broadcasted_iota(jnp.int32, (capacity, tiles), 1).astype(F32)
        chooser = jnp.concatenate(
            [
                (tags[:capacity, source : source + 1] == wide).astype(F32)
                for source in range(cols)
            ],
            axis=0,
        )
        chooser = jnp.transpose(chooser).astype(BF16)
        incoming = jnp.concatenate(
            [
                recv[here, level * capacity : (level + 1) * capacity, :].reshape(
                    cols * capacity, LANES
                )
                for level in range(levels)
            ],
            axis=1,
        )
        high, low = split(incoming)
        total = dot(chooser, high) + dot(chooser, low)
        for level in range(levels):
            sums[level] += total[:, level * LANES : (level + 1) * LANES]

    for offset in (0, 2, 1):
        pl.when(valid(offset))(functools.partial(receive, offset))

    long_tiles, field_rows = field.shape[:2]
    lat_band = field_rows // levels
    shape3 = (levels, long_tiles, LANES)
    lane3 = lax.broadcasted_iota(jnp.int32, shape3, 2)
    inside = lax.broadcasted_iota(jnp.int32, shape3, 1) * LANES + lane3 < longitudes
    for lat in range(lat_band):
        first, shift = divmod(lat * longitudes, LANES)
        value = sums[:, first : first + long_tiles, :]
        if shift:
            after = sums[:, first + 1 : first + 1 + long_tiles, :]
            value = jnp.where(
                lane3 < LANES - shift,
                pltpu.roll(value, LANES - shift, 2),
                pltpu.roll(after, LANES - shift, 2),
            )
        value = jnp.where(inside, value, 0.0)
        for level in range(levels):
            field[:, level * lat_band + lat, :] = value[level]

    rows_wide = jnp.concatenate([field[tile] for tile in range(long_tiles)], axis=1)
    high, low = split(rows_wide)
    both = dot(jnp.concatenate([high, low], axis=0), table_high[...])
    spectrum = both[:field_rows] + both[field_rows:] + dot(high, table_low[...])
    wave_tiles = spectra.shape[2]
    lat_here = lat_band // cols
    for tile in range(wave_tiles):
        spectra[:, :, tile, :] = spectrum[:, tile * LANES : (tile + 1) * LANES].reshape(
            levels, lat_band, LANES
        )

    def lats(ref, index):
        return ref.at[:, pl.ds(index * lat_here, lat_here)]

    def scatter(to):
        pltpu.make_async_remote_copy(
            src_ref=lats(spectra, to),
            dst_ref=arrived.at[col],
            send_sem=scatter_send,
            recv_sem=scatter_recv,
            device_id=(band, to),
            device_id_type=MESH,
        ).start()

    to_others(scatter)
    pltpu.make_async_copy(lats(spectra, col), arrived.at[col], scatter_recv).start()
    remapped[...] = rows_wide[:, :longitudes].reshape(levels, lat_band, longitudes)
    j = (
        lax.broadcasted_iota(jnp.int32, (wave_tiles, LANES), 0) * LANES
        + lax.broadcasted_iota(jnp.int32, (wave_tiles, LANES), 1)
    )
    wave = jnp.where(j >= wave_count, j - wave_count, j)
    weight = jnp.where(wave == 0, 1.0, 2.0) / period
    gains = [jnp.where(wave <= cutoff[lat], weight, 0.0).astype(F32) for lat in range(lat_here)]
    pltpu.make_async_copy(arrived, arrived, scatter_recv).wait()
    for level in range(levels):
        for lat in range(lat_here):
            total = arrived[0, level, lat]
            for source in range(1, cols):
                total += arrived[source, level, lat]
            scaled[level, lat] = total * gains[lat]

    def spread(to):
        pltpu.make_async_remote_copy(
            src_ref=scaled,
            dst_ref=lats(gathered, col),
            send_sem=spread_send,
            recv_sem=spread_recv,
            device_id=(band, to),
            device_id_type=MESH,
        ).start()

    to_others(spread)
    pltpu.make_async_copy(scaled, lats(gathered, col), spread_recv).start()

    def drain(offset):
        count = cols - 1 if offset == 1 else cols
        here = pl.ds(offset * cols, count)
        pltpu.make_async_copy(slab.at[here], recv.at[here], send_sem.at[offset]).wait()

    for offset in range(3):
        pl.when(valid(offset))(functools.partial(drain, offset))
    others = arrived.at[pl.ds(0, cols - 1)]
    pltpu.make_async_copy(others, others, scatter_send).wait()

    pltpu.make_async_copy(spectra, gathered, spread_recv).wait()
    spectrum = jnp.concatenate(
        [gathered[:, :, tile, :].reshape(field_rows, LANES) for tile in range(wave_tiles)], axis=1
    )
    high, low = split(spectrum)
    both = dot(jnp.concatenate([high, low], axis=0), table_high[...], 1, 1)
    result = both[:field_rows] + both[field_rows:] + dot(high, table_low[...], 1, 1)
    filtered[...] = result[:, :longitudes].reshape(levels, lat_band, longitudes)
    pltpu.make_async_copy(others, others, spread_send).wait()


def cos_sin(positions):
    phases = positions[:, None] * np.arange(KW)[None, :] % NLON
    angles = phases * (2 * np.pi / NLON)
    return np.cos(angles).astype(np.float32), np.sin(angles).astype(np.float32)


def local(mesh, source, weights, source_block, owner_device, target_tile, cutoff):
    bands, cols = mesh.shape["band"], mesh.shape["col"]
    levels = source.shape[0]
    block_count, block_width = weights.shape[:2]
    lat_here = cutoff.shape[0]
    lat_band = lat_here * cols
    longitudes = NLON // cols
    cell_count = lat_band * longitudes
    tile_count = (cell_count + block_width - 1) // block_width
    regular = (tile_count + cols - 1) // cols
    capacity = regular + max(1, (block_count - cols * regular + 2 * cols - 1) // (2 * cols))
    capacity = round_up(capacity, 8)
    long_pad = round_up(longitudes, LANES)
    long_tiles = long_pad // LANES
    tiles = round_up(tile_count + long_tiles, LANES)
    fine = np.stack(cos_sin(np.arange(STEP)))
    coarse = np.stack(cos_sin(STEP * np.arange(long_pad // STEP)), axis=1)
    start = np.stack(cos_sin(longitudes * np.arange(cols)), axis=1)

    blocks_here = source.reshape(levels, -1, block_width)
    picked = blocks_here.at[:, source_block].get(mode="promise_in_bounds")
    partial = jnp.einsum("lnb,nbt->nlt", picked, weights, preferred_element_type=F32)
    slab_rows = levels * capacity + 8
    wave_tiles = 2 * KW // LANES
    vmem = pl.BlockSpec(memory_space=pltpu.VMEM)
    shape = jax.ShapeDtypeStruct((levels, lat_band, longitudes), F32)
    return pl.pallas_call(
        functools.partial(remap_kernel, bands, cols, levels, capacity, KW, NLON, longitudes),
        out_shape=(shape, shape),
        in_specs=[pl.BlockSpec(memory_space=pltpu.SMEM)] + [vmem] * 7,
        out_specs=(vmem, vmem),
        scratch_shapes=[
            pltpu.VMEM((levels, tiles, LANES), F32),
            pltpu.VMEM((long_pad, 2 * KW), BF16),
            pltpu.VMEM((long_pad, 2 * KW), BF16),
            pltpu.VMEM((2, STEP, KW), F32),
            pltpu.VMEM((long_tiles, levels * lat_band, LANES), F32),
            pltpu.VMEM((3 * cols, slab_rows, LANES), F32),
            pltpu.VMEM((3 * cols, slab_rows, LANES), F32),
            pltpu.VMEM((levels, lat_band, wave_tiles, LANES), F32),
            pltpu.VMEM((cols, levels, lat_here, wave_tiles, LANES), F32),
            pltpu.VMEM((levels, lat_here, wave_tiles, LANES), F32),
            pltpu.VMEM((levels, lat_band, wave_tiles, LANES), F32),
            pltpu.SemaphoreType.DMA((3,)),
            pltpu.SemaphoreType.DMA((3,)),
            pltpu.SemaphoreType.DMA,
            pltpu.SemaphoreType.DMA,
            pltpu.SemaphoreType.DMA,
            pltpu.SemaphoreType.DMA,
        ],
        compiler_params=pltpu.CompilerParams(has_side_effects=True, vmem_limit_bytes=48 << 20),
    )(
        cutoff,
        partial,
        owner_device.reshape(1, block_count),
        owner_device,
        target_tile.reshape(1, block_count),
        fine,
        coarse,
        start,
    )


def solution(mesh):
    in_specs = (
        P(None, ("band", "col")),
        P(("band", "col"), None, None),
        P(("band", "col")),
        P(("band", "col"), None),
        P(("band", "col")),
        P(("band", "col")),
    )
    out_specs = (P(None, "band", "col"), P(None, "band", "col"))
    return jax.shard_map(
        functools.partial(local, mesh),
        mesh=mesh,
        in_specs=in_specs,
        out_specs=out_specs,
        check_vma=False,
    )
```

time: 95.9 us -> 76.3 us (0.80)
  Pallas kernels: 74 us -> 65.1 us
  other arithmetic: 5.7 us -> 0.69 us
  local copies, waits for them, and re-layouts: 8.89 us -> 4.05 us
    pallas_call x2 -> x1, Pallas kernels: 74 us -> 65.1 us  [local(): pl.pallas_call(functools.partial(remap_kernel, bands, cols, levels, capac...]
    cos x1 -> x0, other arithmetic: 3.78 us -> none  [cos_sin(): return (jnp.cos(angles), jnp.sin(angles))]
    reshape x4 -> x0, local copies, waits for them, and re-layouts: 2.62 us -> none  [the longest x1 1.08 us: local(): sums.reshape(levels, -1)[:, :cell_count]]
    unnamed x14 -> x17, local copies, waits for them, and re-layouts: 4.9 us -> 3.22 us
where the time goes in v2:
time: 76.3 us; the launch traced here: 75.2 us
  Pallas kernels  65.1 us (85%)
  matrix products  4.66 us (6%)
  local copies, waits for them, and re-layouts  4.05 us (5%)
    pallas_call x1, Pallas kernels, local(): pl.pallas_call(functools.partial(remap_kernel, bands, cols, levels, capac...  65.1 us
    dot_general x1, matrix products, local(): jnp.einsum('lnb,nbt->nlt', picked, weights, preferred_element_type=F32)  4.66 us
    unnamed x17, local copies, waits for them, and re-layouts  3.22 us

profile of v2, /device:TPU:4, one launch (start us, length us, event | category | flops | bytes accessed | tf_op | source)
XLA Modules:
  0.0 75.2 jit_solution(9504352594330909261)
XLA Ops:
  0.6 0.0 copy-start
  0.6 0.0 copy-start.3
  0.7 0.0 copy-start.1
  0.7 0.0 copy-start.2
  0.7 0.0 copy-start.4
  0.7 0.0 copy-start.6
  0.7 0.0 copy-start.5
  0.7 0.9 %copy-done = bf16[6,16384]{1,0:T(8,128)(2,1)S(1)} copy-done((bf16[6,16384]{1,0:T(8,128)(2,1)S(1)}, bf16[6,16384]{1,0:T(8,128)(2,1)}, u32[]{:S(2)}) %copy-start) | copy-done | bytes 196632
  1.6 0.7 compare_select_fusion
  2.3 0.8 %copy.12.owner_column = s32[256,1]{1,0:T(8,128)S(1)} copy(s32[256,1]{0,1:T(1,128)} %param.12) | data formatting | bytes 2048 | tf_op args[3]
  3.1 0.8 %gather_fusion = bf16[256,6,128]{2,1,0:T(8,128)(2,1)S(1)} fusion(bf16[6,128,128]{2,0,1:T(8,128)(2,1)S(1)} %bitcast.7, s32[1024]{0:T(1024)S(1)} %pad_clamp_fusion), kind=kCustom, calls=%fused_computation | custom fusion | bytes 787456 | tf_op jit(solution)/shard_map/gather | solution.py:282
  3.9 4.7 %fusion.partial = f32[256,6,128]{2,1,0:T(8,128)S(1)} fusion(bf16[256,128,128]{2,1,0:T(8,128)(2,1)} %param.10, bf16[256,6,128]{2,1,0:T(8,128)(2,1)S(1)} %gather_fusion), kind=kOutput, calls=%fused_computation.1 | convolution fusion | flops 50331648 | bytes 9568256 | tf_op jit(solution)/shard_map/lnb,nbt->nlt/dot_general | solution.py:283
  8.6 0.0 copy-done.3
  8.6 0.0 copy-done.1
  8.6 0.0 copy-done.2
  8.6 0.0 copy-done.4
  8.6 0.0 copy-done.6
  8.6 0.0 copy-done.5
  8.6 65.1 %shard_map.104 = (f32[6,16,900]{2,1,0:T(8,128)S(1)}, f32[6,16,900]{2,1,0:T(8,128)S(1)}) custom-call(s32[2]{0:T(128)S(1)} %copy-done.6, f32[256,6,128]{2,1,0:T(8,128)S(1)} %fusion.partial, s32[1,256]{1,0:T(1,128)S(1)} %bitcast.8, s32[256,1]{1,0:T(8,128)S(1)} %copy.12.owner_column, s32[1,256]{1,0:T(1,128)S(1)} %bitcast.9, f32[2,16,512]{2,1,0:T(8,128)S(1)} %copy-done.2, ...), custom_call_target="tpu_custom_call" | custom-call | tf_op jit(solution)/shard_map/pallas_call | solution.py:288
  73.7 0.7 copy.15
  74.5 0.7 copy.16
  (1 shorter events, 0.0 us)
Async XLA Ops:
  0.6 1.0 %copy-start = (bf16[6,16384]{1,0:T(8,128)(2,1)S(1)}, bf16[6,16384]{1,0:T(8,128)(2,1)}, u32[]{:S(2)}) copy-start(bf16[6,16384]{1,0:T(8,128)(2,1)} %param.9) | copy-start | bytes 589828
  0.6 7.9 %copy-start.3 = (f32[8,2,512]{2,1,0:T(2,128)S(1)}, f32[8,2,512]{2,1,0:T(2,128)}, u32[]{:S(2)}) copy-start(f32[8,2,512]{2,1,0:T(2,128)} %constant.12.clone.start) | copy-start | bytes 98308
  0.7 7.9 %copy-start.1 = (f32[64,2,512]{2,1,0:T(2,128)S(1)}, f32[64,2,512]{2,1,0:T(2,128)}, u32[]{:S(2)}) copy-start(f32[64,2,512]{2,1,0:T(2,128)} %constant.11.clone.coarse) | copy-start | bytes 786436
  0.7 7.9 %copy-start.2 = (f32[2,16,512]{2,1,0:T(8,128)S(1)}, f32[2,16,512]{2,1,0:T(8,128)}, u32[]{:S(2)}) copy-start(f32[2,16,512]{2,1,0:T(8,128)} %constant.10.clone.fine) | copy-start | bytes 196612
  0.7 7.9 %copy-start.4 = (s32[256,1]{0,1:T(1,128)S(1)}, s32[256,1]{0,1:T(1,128)}, u32[]{:S(2)}) copy-start(s32[256,1]{0,1:T(1,128)} %param.12) | copy-start | bytes 3076
  0.7 7.9 %copy-start.6 = (s32[2]{0:T(128)S(1)}, s32[2]{0:T(128)}, u32[]{:S(2)}) copy-start(s32[2]{0:T(128)} %cutoff.1) | copy-start | bytes 28
  0.7 7.9 %copy-start.5 = (s32[256]{0:T(256)S(1)}, s32[256]{0:T(256)}, u32[]{:S(2)}) copy-start(s32[256]{0:T(256)} %param.13) | copy-start | bytes 3076

commit v3 on v2

--- a/solution.py
+++ b/solution.py
@@ -33,12 +33,13 @@
 
 
 def remap_kernel(
-    bands, cols, levels, capacity, wave_count, period, longitudes,
-    cutoff, partial, owner_row, owner_column, tile_row, fine, coarse, start,
+    bands, cols, levels, capacity, wave_count, period, longitudes, tile_count,
+    cutoff, partial, owner_row, tile_row, fine, coarse, start,
     remapped, filtered,
-    sums, table_high, table_low, rotated, field, slab, recv,
+    sums, table_high, table_low, rotated, field, slab, recv, relay, relay_sums, passed,
     spectra, arrived, scaled, gathered,
-    send_sem, recv_sem, scatter_send, scatter_recv, spread_send, spread_recv,
+    send_sem, recv_sem, relay_sem, pass_send, pass_recv,
+    scatter_send, scatter_recv, spread_send, spread_recv,
 ):
     band, col = lax.axis_index("band"), lax.axis_index("col")
     blocks = partial.shape[0]
@@ -46,7 +47,9 @@
     owners = owner_row[...]
     sublane = lax.broadcasted_iota(jnp.int32, (blocks, blocks), 0)
     lane = lax.broadcasted_iota(jnp.int32, (blocks, blocks), 1)
-    earlier = (owner_column[...] == owners) & (sublane < lane)
+    owners_wide = jnp.broadcast_to(owners.astype(F32), (8, blocks))
+    owner_column = jnp.transpose(owners_wide)[:, 0:1]
+    earlier = (owner_column == owners.astype(F32)) & (sublane < lane)
     rank = jnp.sum(earlier.astype(jnp.int32), axis=0, keepdims=True)
     place = owners - (band - 1) * cols
     slot = place * capacity + rank
@@ -83,26 +86,47 @@
             )
         slab[here, rows : rows + 8, :] = jnp.broadcast_to(tags[:, None, :], (cols, 8, LANES))
 
-        def start_remote(to):
-            pltpu.make_async_remote_copy(
-                src_ref=slab.at[offset * cols + to],
-                dst_ref=recv.at[(2 - offset) * cols + col],
-                send_sem=send_sem.at[offset],
-                recv_sem=recv_sem.at[2 - offset],
-                device_id=(band + (offset - 1), to),
-                device_id_type=MESH,
-            ).start()
-
-        to_others(start_remote)
+    half_size = cols // 2
+    half, place_in_half = col // half_size, lax.rem(col, half_size)
+
+    def push(owner_half, into, sems, offset):
+        def one(step, carry):
+            to = lax.rem(place_in_half + half_size // 2 + step, half_size)
+            source = slab.at[offset * cols + owner_half * half_size + to]
+            target = into.at[(2 - offset) * half_size + place_in_half]
+
+            def start_remote():
+                pltpu.make_async_remote_copy(
+                    src_ref=source,
+                    dst_ref=target,
+                    send_sem=send_sem.at[offset],
+                    recv_sem=sems.at[2 - offset],
+                    device_id=(band + (offset - 1), half * half_size + to),
+                    device_id_type=MESH,
+                ).start()
+
+            if offset == 1:
+                pl.when(to != place_in_half)(start_remote)
+            else:
+                start_remote()
+            return carry
+
+        lax.fori_loop(0, half_size, one, 0)
         if offset == 1:
             pltpu.make_async_copy(
-                slab.at[cols + col], recv.at[cols + col], recv_sem.at[1]
+                slab.at[cols + owner_half * half_size + place_in_half],
+                into.at[half_size + place_in_half],
+                sems.at[1],
             ).start()
-        else:
-            start_remote(col)
+
+    def place_and_push(offset):
+        send(offset)
+        push(1 - half, relay, relay_sem, offset)
 
     for offset in (0, 2, 1):
-        pl.when(valid(offset))(functools.partial(send, offset))
+        pl.when(valid(offset))(functools.partial(place_and_push, offset))
+    for offset in (0, 2, 1):
+        pl.when(valid(offset))(functools.partial(push, half, recv, recv_sem, offset))
 
     begin = start[col]
     cos_start, sin_start = begin[0:1], begin[1:2]
@@ -127,24 +151,27 @@
 
     tiles = sums.shape[1]
     sums[...] = jnp.zeros_like(sums)
-
-    def receive(offset):
-        here = pl.ds(offset * cols, cols)
-        pltpu.make_async_copy(slab.at[here], recv.at[here], recv_sem.at[offset]).wait()
-        tags = jnp.transpose(recv[here, rows, :])
+    relay_sums[...] = jnp.zeros_like(relay_sums)
+
+    def receive(ref, sems, into, offset):
+        here = pl.ds(offset * half_size, half_size)
+        pltpu.make_async_copy(ref.at[here], ref.at[here], sems.at[offset]).wait()
+        tags = jnp.transpose(
+            jnp.concatenate([ref[here, rows, :]] * (-(-8 // half_size)), axis=0)
+        )
         wide = lax.broadcasted_iota(jnp.int32, (capacity, tiles), 1).astype(F32)
         chooser = jnp.concatenate(
             [
                 (tags[:capacity, source : source + 1] == wide).astype(F32)
-                for source in range(cols)
+                for source in range(half_size)
             ],
             axis=0,
         )
         chooser = jnp.transpose(chooser).astype(BF16)
         incoming = jnp.concatenate(
             [
-                recv[here, level * capacity : (level + 1) * capacity, :].reshape(
-                    cols * capacity, LANES
+                ref[here, level * capacity : (level + 1) * capacity, :].reshape(
+                    half_size * capacity, LANES
                 )
                 for level in range(levels)
             ],
@@ -153,10 +180,24 @@
         high, low = split(incoming)
         total = dot(chooser, high) + dot(chooser, low)
         for level in range(levels):
-            sums[level] += total[:, level * LANES : (level + 1) * LANES]
+            into[level] += total[:, level * LANES : (level + 1) * LANES]
 
     for offset in (0, 2, 1):
-        pl.when(valid(offset))(functools.partial(receive, offset))
+        pl.when(valid(offset))(functools.partial(receive, relay, relay_sem, relay_sums, offset))
+    dense = pl.ds(0, tile_count)
+    dense_copy = pltpu.make_async_remote_copy(
+        src_ref=relay_sums.at[:, dense],
+        dst_ref=passed,
+        send_sem=pass_send,
+        recv_sem=pass_recv,
+        device_id=(band, (1 - half) * half_size + place_in_half),
+        device_id_type=MESH,
+    )
+    dense_copy.start()
+    for offset in (0, 2, 1):
+        pl.when(valid(offset))(functools.partial(receive, recv, recv_sem, sums, offset))
+    dense_copy.wait()
+    sums[:, :tile_count, :] += passed[...]
 
     long_tiles, field_rows = field.shape[:2]
     lat_band = field_rows // levels
@@ -233,9 +274,8 @@
     pltpu.make_async_copy(scaled, lats(gathered, col), spread_recv).start()
 
     def drain(offset):
-        count = cols - 1 if offset == 1 else cols
-        here = pl.ds(offset * cols, count)
-        pltpu.make_async_copy(slab.at[here], recv.at[here], send_sem.at[offset]).wait()
+        sent = slab.at[pl.ds(0, cols - 2 if offset == 1 else cols)]
+        pltpu.make_async_copy(sent, sent, send_sem.at[offset]).wait()
 
     for offset in range(3):
         pl.when(valid(offset))(functools.partial(drain, offset))
@@ -279,16 +319,16 @@
     start = np.stack(cos_sin(longitudes * np.arange(cols)), axis=1)
 
     blocks_here = source.reshape(levels, -1, block_width)
-    picked = blocks_here.at[:, source_block].get(mode="promise_in_bounds")
+    picked = blocks_here.at[:, source_block.astype(jnp.uint32)].get(mode="promise_in_bounds")
     partial = jnp.einsum("lnb,nbt->nlt", picked, weights, preferred_element_type=F32)
     slab_rows = levels * capacity + 8
     wave_tiles = 2 * KW // LANES
     vmem = pl.BlockSpec(memory_space=pltpu.VMEM)
     shape = jax.ShapeDtypeStruct((levels, lat_band, longitudes), F32)
     return pl.pallas_call(
-        functools.partial(remap_kernel, bands, cols, levels, capacity, KW, NLON, longitudes),
+        functools.partial(remap_kernel, bands, cols, levels, capacity, KW, NLON, longitudes, round_up(tile_count, 8)),
         out_shape=(shape, shape),
-        in_specs=[pl.BlockSpec(memory_space=pltpu.SMEM)] + [vmem] * 7,
+        in_specs=[pl.BlockSpec(memory_space=pltpu.SMEM)] + [vmem] * 6,
         out_specs=(vmem, vmem),
         scratch_shapes=[
             pltpu.VMEM((levels, tiles, LANES), F32),
@@ -297,13 +337,19 @@
             pltpu.VMEM((2, STEP, KW), F32),
             pltpu.VMEM((long_tiles, levels * lat_band, LANES), F32),
             pltpu.VMEM((3 * cols, slab_rows, LANES), F32),
-            pltpu.VMEM((3 * cols, slab_rows, LANES), F32),
+            pltpu.VMEM((3 * cols // 2, slab_rows, LANES), F32),
+            pltpu.VMEM((3 * cols // 2, slab_rows, LANES), F32),
+            pltpu.VMEM((levels, tiles, LANES), F32),
+            pltpu.VMEM((levels, round_up(tile_count, 8), LANES), F32),
             pltpu.VMEM((levels, lat_band, wave_tiles, LANES), F32),
             pltpu.VMEM((cols, levels, lat_here, wave_tiles, LANES), F32),
             pltpu.VMEM((levels, lat_here, wave_tiles, LANES), F32),
             pltpu.VMEM((levels, lat_band, wave_tiles, LANES), F32),
             pltpu.SemaphoreType.DMA((3,)),
             pltpu.SemaphoreType.DMA((3,)),
+            pltpu.SemaphoreType.DMA((3,)),
+            pltpu.SemaphoreType.DMA,
+            pltpu.SemaphoreType.DMA,
             pltpu.SemaphoreType.DMA,
             pltpu.SemaphoreType.DMA,
             pltpu.SemaphoreType.DMA,
@@ -314,7 +360,6 @@
         cutoff,
         partial,
         owner_device.reshape(1, block_count),
-        owner_device,
         target_tile.reshape(1, block_count),
         fine,
         coarse,

time: 76.3 us -> 68.8 us (0.902)
  the two profiles are of different devices: /device:TPU:4 before, /device:TPU:25 now
where the time goes in v3:
time: 68.8 us; the launch traced here: 68.6 us
  Pallas kernels  59.3 us (86%)
  matrix products  4.66 us (7%)
  local copies, waits for them, and re-layouts  3.24 us (5%)
  between operations  0.73 us (1%)
  other arithmetic  0.69 us (1%)
    pallas_call x1, Pallas kernels, local(): pl.pallas_call(functools.partial(remap_kernel, bands, cols, levels, capac...  59.3 us
    dot_general x1, matrix products, local(): jnp.einsum('lnb,nbt->nlt', picked, weights, preferred_element_type=F32)  4.66 us
    unnamed x16, local copies, waits for them, and re-layouts  2.42 us

profile of v3, /device:TPU:25, one launch (start us, length us, event | category | flops | bytes accessed | tf_op | source)
XLA Modules:
  0.0 68.6 jit_solution(8834959884635391369)
XLA Ops:
  0.6 0.0 copy-start
  0.6 0.0 copy-start.3
  0.7 0.0 copy-start.1
  0.7 0.0 copy-start.2
  0.7 0.0 copy-start.6
  0.7 0.0 copy-start.5
  0.7 0.0 copy-start.4
  0.7 0.9 %copy-done = bf16[6,16384]{1,0:T(8,128)(2,1)S(1)} copy-done((bf16[6,16384]{1,0:T(8,128)(2,1)S(1)}, bf16[6,16384]{1,0:T(8,128)(2,1)}, u32[]{:S(2)}) %copy-start) | copy-done | bytes 196632
  1.6 0.7 convert_convert_fusion
  2.3 0.8 %gather_fusion = bf16[256,6,128]{2,1,0:T(8,128)(2,1)S(1)} fusion(bf16[6,128,128]{2,0,1:T(8,128)(2,1)S(1)} %bitcast.7, s32[1024]{0:T(1024)S(1)} %pad_clamp_fusion), kind=kCustom, calls=%fused_computation | custom fusion | bytes 787456 | tf_op jit(solution)/shard_map/gather | solution.py:322
  3.1 4.7 %fusion.partial = f32[256,6,128]{2,1,0:T(8,128)S(1)} fusion(bf16[256,128,128]{2,1,0:T(8,128)(2,1)} %param.10, bf16[256,6,128]{2,1,0:T(8,128)(2,1)S(1)} %gather_fusion), kind=kOutput, calls=%fused_computation.1 | convolution fusion | flops 50331648 | bytes 9568256 | tf_op jit(solution)/shard_map/lnb,nbt->nlt/dot_general | solution.py:323
  7.8 0.0 copy-done.3
  7.8 0.0 copy-done.1
  7.8 0.0 copy-done.2
  7.8 0.0 copy-done.6
  7.8 0.0 copy-done.5
  7.8 0.0 copy-done.4
  7.8 59.3 %shard_map.104 = (f32[6,16,900]{2,1,0:T(8,128)S(1)}, f32[6,16,900]{2,1,0:T(8,128)S(1)}) custom-call(s32[2]{0:T(128)S(1)} %copy-done.6, f32[256,6,128]{2,1,0:T(8,128)S(1)} %fusion.partial, s32[1,256]{1,0:T(1,128)S(1)} %bitcast.8, s32[1,256]{1,0:T(1,128)S(1)} %bitcast.9, f32[2,16,512]{2,1,0:T(8,128)S(1)} %copy-done.2, f32[64,2,512]{2,1,0:T(2,128)S(1)} %copy-done.1, ...), custom_call_target="tpu_custom_call" | custom-call | tf_op jit(solution)/shard_map/pallas_call | solution.py:328
  67.1 0.7 %copy.13 = f32[6,16,900]{2,1,0:T(8,128)} copy(f32[6,16,900]{2,1,0:T(8,128)S(1)} %get-tuple-element.4) | data formatting | bytes 691200
  67.9 0.7 %copy.14 = f32[6,16,900]{2,1,0:T(8,128)} copy(f32[6,16,900]{2,1,0:T(8,128)S(1)} %get-tuple-element.5) | data formatting | bytes 691200
  (1 shorter events, 0.0 us)
Async XLA Ops:
  0.6 1.0 %copy-start = (bf16[6,16384]{1,0:T(8,128)(2,1)S(1)}, bf16[6,16384]{1,0:T(8,128)(2,1)}, u32[]{:S(2)}) copy-start(bf16[6,16384]{1,0:T(8,128)(2,1)} %param.9) | copy-start | bytes 589828
  0.6 7.1 %copy-start.3 = (f32[8,2,512]{2,1,0:T(2,128)S(1)}, f32[8,2,512]{2,1,0:T(2,128)}, u32[]{:S(2)}) copy-start(f32[8,2,512]{2,1,0:T(2,128)} %constant.8.clone.start) | copy-start | bytes 98308
  0.7 7.1 %copy-start.1 = (f32[64,2,512]{2,1,0:T(2,128)S(1)}, f32[64,2,512]{2,1,0:T(2,128)}, u32[]{:S(2)}) copy-start(f32[64,2,512]{2,1,0:T(2,128)} %constant.7.clone.coarse) | copy-start | bytes 786436
  0.7 7.1 %copy-start.2 = (f32[2,16,512]{2,1,0:T(8,128)S(1)}, f32[2,16,512]{2,1,0:T(8,128)}, u32[]{:S(2)}) copy-start(f32[2,16,512]{2,1,0:T(8,128)} %constant.6.clone.fine) | copy-start | bytes 196612
  0.7 7.1 %copy-start.6 = (s32[2]{0:T(128)S(1)}, s32[2]{0:T(128)}, u32[]{:S(2)}) copy-start(s32[2]{0:T(128)} %cutoff.1) | copy-start | bytes 28
  0.7 7.1 %copy-start.5 = (s32[256]{0:T(256)S(1)}, s32[256]{0:T(256)}, u32[]{:S(2)}) copy-start(s32[256]{0:T(256)} %param.13) | copy-start | bytes 3076
  0.7 7.1 %copy-start.4 = (s32[256,1]{0,1:T(1,128)S(1)}, s32[256,1]{0,1:T(1,128)}, u32[]{:S(2)}) copy-start(s32[256,1]{0,1:T(1,128)} %param.12) | copy-start | bytes 3076

commit v4 on v3

--- a/solution.py
+++ b/solution.py
@@ -39,7 +39,7 @@
     sums, table_high, table_low, rotated, field, slab, recv, relay, relay_sums, passed,
     spectra, arrived, scaled, gathered,
     send_sem, recv_sem, relay_sem, pass_send, pass_recv,
-    scatter_send, scatter_recv, spread_send, spread_recv,
+    scatter_send, scatter_recv, spread_send, spread_recv, cross_recv,
 ):
     band, col = lax.axis_index("band"), lax.axis_index("col")
     blocks = partial.shape[0]
@@ -260,18 +260,41 @@
                 total += arrived[source, level, lat]
             scaled[level, lat] = total * gains[lat]
 
-    def spread(to):
+    twin_half = (1 - half) * half_size
+
+    def spread(source, owner, to):
         pltpu.make_async_remote_copy(
-            src_ref=scaled,
-            dst_ref=lats(gathered, col),
+            src_ref=source,
+            dst_ref=lats(gathered, owner),
             send_sem=spread_send,
             recv_sem=spread_recv,
             device_id=(band, to),
             device_id_type=MESH,
         ).start()
 
-    to_others(spread)
+    def to_half(source, owner):
+        def one(step, carry):
+            to = lax.rem(place_in_half + half_size // 2 + step, half_size)
+            pl.when(to != place_in_half)(
+                lambda: spread(source, owner, half * half_size + to)
+            )
+            return carry
+
+        lax.fori_loop(0, half_size, one, 0)
+
+    pltpu.make_async_remote_copy(
+        src_ref=scaled,
+        dst_ref=lats(gathered, col),
+        send_sem=spread_send,
+        recv_sem=cross_recv,
+        device_id=(band, twin_half + place_in_half),
+        device_id_type=MESH,
+    ).start()
+    to_half(scaled, col)
     pltpu.make_async_copy(scaled, lats(gathered, col), spread_recv).start()
+    twin = twin_half + place_in_half
+    pltpu.make_async_copy(scaled, lats(gathered, twin), cross_recv).wait()
+    to_half(lats(gathered, twin), twin)
 
     def drain(offset):
         sent = slab.at[pl.ds(0, cols - 2 if offset == 1 else cols)]
@@ -282,7 +305,7 @@
     others = arrived.at[pl.ds(0, cols - 1)]
     pltpu.make_async_copy(others, others, scatter_send).wait()
 
-    pltpu.make_async_copy(spectra, gathered, spread_recv).wait()
+    pltpu.make_async_copy(others, others, spread_recv).wait()
     spectrum = jnp.concatenate(
         [gathered[:, :, tile, :].reshape(field_rows, LANES) for tile in range(wave_tiles)], axis=1
     )
@@ -354,6 +377,7 @@
             pltpu.SemaphoreType.DMA,
             pltpu.SemaphoreType.DMA,
             pltpu.SemaphoreType.DMA,
+            pltpu.SemaphoreType.DMA,
         ],
         compiler_params=pltpu.CompilerParams(has_side_effects=True, vmem_limit_bytes=48 << 20),
     )(

time: 68.8 us -> 68.9 us (level)
  the two profiles are of different devices: /device:TPU:25 before, /device:TPU:4 now
where the time goes in v4:
time: 68.9 us; the launch traced here: 68.7 us
  Pallas kernels  59.4 us (86%)
  matrix products  4.66 us (7%)
  local copies, waits for them, and re-layouts  3.24 us (5%)
  between operations  0.73 us (1%)
  other arithmetic  0.69 us (1%)
    pallas_call x1, Pallas kernels, local(): pl.pallas_call(functools.partial(remap_kernel, bands, cols, levels, capac...  59.4 us
    dot_general x1, matrix products, local(): jnp.einsum('lnb,nbt->nlt', picked, weights, preferred_element_type=F32)  4.66 us
    unnamed x16, local copies, waits for them, and re-layouts  2.42 us

profile of v4, /device:TPU:4, one launch (start us, length us, event | category | flops | bytes accessed | tf_op | source)
XLA Modules:
  0.0 68.7 jit_solution(12295989624424972715)
XLA Ops:
  0.6 0.0 copy-start
  0.6 0.0 copy-start.3
  0.7 0.0 copy-start.1
  0.7 0.0 copy-start.2
  0.7 0.0 copy-start.6
  0.7 0.0 copy-start.5
  0.7 0.0 copy-start.4
  0.7 0.9 %copy-done = bf16[6,16384]{1,0:T(8,128)(2,1)S(1)} copy-done((bf16[6,16384]{1,0:T(8,128)(2,1)S(1)}, bf16[6,16384]{1,0:T(8,128)(2,1)}, u32[]{:S(2)}) %copy-start) | copy-done | bytes 196632
  1.6 0.7 convert_convert_fusion
  2.3 0.8 %gather_fusion = bf16[256,6,128]{2,1,0:T(8,128)(2,1)S(1)} fusion(bf16[6,128,128]{2,0,1:T(8,128)(2,1)S(1)} %bitcast.7, s32[1024]{0:T(1024)S(1)} %pad_clamp_fusion), kind=kCustom, calls=%fused_computation | custom fusion | bytes 787456 | tf_op jit(solution)/shard_map/gather | solution.py:345
  3.1 4.7 %fusion.partial = f32[256,6,128]{2,1,0:T(8,128)S(1)} fusion(bf16[256,128,128]{2,1,0:T(8,128)(2,1)} %param.10, bf16[256,6,128]{2,1,0:T(8,128)(2,1)S(1)} %gather_fusion), kind=kOutput, calls=%fused_computation.1 | convolution fusion | flops 50331648 | bytes 9568256 | tf_op jit(solution)/shard_map/lnb,nbt->nlt/dot_general | solution.py:346
  7.8 0.0 copy-done.3
  7.8 0.0 copy-done.1
  7.8 0.0 copy-done.2
  7.8 0.0 copy-done.6
  7.8 0.0 copy-done.5
  7.8 0.0 copy-done.4
  7.8 59.4 %shard_map.104 = (f32[6,16,900]{2,1,0:T(8,128)S(1)}, f32[6,16,900]{2,1,0:T(8,128)S(1)}) custom-call(s32[2]{0:T(128)S(1)} %copy-done.6, f32[256,6,128]{2,1,0:T(8,128)S(1)} %fusion.partial, s32[1,256]{1,0:T(1,128)S(1)} %bitcast.8, s32[1,256]{1,0:T(1,128)S(1)} %bitcast.9, f32[2,16,512]{2,1,0:T(8,128)S(1)} %copy-done.2, f32[64,2,512]{2,1,0:T(2,128)S(1)} %copy-done.1, ...), custom_call_target="tpu_custom_call" | custom-call | tf_op jit(solution)/shard_map/pallas_call | solution.py:351
  67.2 0.7 %copy.13 = f32[6,16,900]{2,1,0:T(8,128)} copy(f32[6,16,900]{2,1,0:T(8,128)S(1)} %get-tuple-element.4) | data formatting | bytes 691200
  68.0 0.7 %copy.14 = f32[6,16,900]{2,1,0:T(8,128)} copy(f32[6,16,900]{2,1,0:T(8,128)S(1)} %get-tuple-element.5) | data formatting | bytes 691200
  (1 shorter events, 0.0 us)
Async XLA Ops:
  0.6 1.0 %copy-start = (bf16[6,16384]{1,0:T(8,128)(2,1)S(1)}, bf16[6,16384]{1,0:T(8,128)(2,1)}, u32[]{:S(2)}) copy-start(bf16[6,16384]{1,0:T(8,128)(2,1)} %param.9) | copy-start | bytes 589828
  0.6 7.1 %copy-start.3 = (f32[8,2,512]{2,1,0:T(2,128)S(1)}, f32[8,2,512]{2,1,0:T(2,128)}, u32[]{:S(2)}) copy-start(f32[8,2,512]{2,1,0:T(2,128)} %constant.8.clone.start) | copy-start | bytes 98308
  0.7 7.1 %copy-start.1 = (f32[64,2,512]{2,1,0:T(2,128)S(1)}, f32[64,2,512]{2,1,0:T(2,128)}, u32[]{:S(2)}) copy-start(f32[64,2,512]{2,1,0:T(2,128)} %constant.7.clone.coarse) | copy-start | bytes 786436
  0.7 7.1 %copy-start.2 = (f32[2,16,512]{2,1,0:T(8,128)S(1)}, f32[2,16,512]{2,1,0:T(8,128)}, u32[]{:S(2)}) copy-start(f32[2,16,512]{2,1,0:T(8,128)} %constant.6.clone.fine) | copy-start | bytes 196612
  0.7 7.1 %copy-start.6 = (s32[2]{0:T(128)S(1)}, s32[2]{0:T(128)}, u32[]{:S(2)}) copy-start(s32[2]{0:T(128)} %cutoff.1) | copy-start | bytes 28
  0.7 7.1 %copy-start.5 = (s32[256]{0:T(256)S(1)}, s32[256]{0:T(256)}, u32[]{:S(2)}) copy-start(s32[256]{0:T(256)} %param.13) | copy-start | bytes 3076
  0.7 7.1 %copy-start.4 = (s32[256,1]{0,1:T(1,128)S(1)}, s32[256,1]{0,1:T(1,128)}, u32[]{:S(2)}) copy-start(s32[256,1]{0,1:T(1,128)} %param.12) | copy-start | bytes 3076
